TPU v7x, 256 devices: a whole 4x4x8 slice. The times are simulated.
256 devices in a mesh: row: 32 (over x, z_hi, y), col: 8 (over z_lo, core).
Axes of the slice: x: 4, y: 4, z: 8 (z_hi: 2, z_lo: 4; z = z_hi * 4 + z_lo), core: 2. Of those that a mesh axis runs over, the one named last changes fastest.
Arguments:
- lanczos_now: float32 [1, 256, 1024], P(None, 'row', 'col'), may hold values from -80 to 80, as said below
- lanczos_prev: float32 [1, 256, 1024], P(None, 'row', 'col'), may hold values from -6 to 6
- beta_prev: float32 [1], replicated, may hold values from 0.3 to 1.5
- valence_energy: float32 [256], P('row'), may hold values from -1.5 to -0.5
- conduction_energy: float32 [1024], P('col'), may hold values from 0.5 to 2.5
- valence_panel: float32 [16384, 256], P(('row', 'col')), may hold values from -0.375 to 0.375
- conduction_panel: float32 [16384, 1024], P(('row', 'col')), may hold values from -0.1875 to 0.1875
- screened_coulomb: float32 [16384, 16384], P('row', 'col'), may hold values from -0.046875 to 0.046875
- bare_coulomb: float32 [16384, 16384], P('row', 'col'), may hold values from -0.046875 to 0.046875
Outputs:
- lanczos_next: float32 [1, 256, 1024], P(None, 'row', 'col')
- coefficients: float32 [1, 2], replicated
Inputs may be any that keep to these rules, and one draw needn't show every extreme that they name: `lanczos_now`: real entries; the vectors of a chain are not normalized.
All inputs are finite; a program needn't handle non-finite values.
Results may differ from a plain program's by a relative error of at most 0.0002.
Values sent between devices are 32-bit elements; how exact they have to be, the bound alone decides.
A program may use at most 128 MiB of HBM per device.

v0:
```python
import jax
import jax.numpy as jnp
from jax import lax
from jax.sharding import Mesh
from jax.sharding import PartitionSpec as P

V = 256
C = 1024
COL = ("col_0", "col_1")
ROW = ("row_0", "row_1", "row_2")
ROW_COL = ("row_0", "row_1", "row_2", "col_0", "col_1")
precise = lax.Precision.HIGHEST
epsilon = 1e-06


def copy_for_each(shard, axis):
    copies = jnp.broadcast_to(shard, (lax.axis_size(axis), *shard.shape))
    return lax.all_to_all(copies, axis, split_axis=0, concat_axis=0, tiled=True)


def joined_along(parts, dim):
    dims = list(parts.shape[1:])
    dims[dim] *= parts.shape[0]
    return jnp.moveaxis(parts, 0, dim).reshape(dims)


def gather_directly(shard, axis, dim):
    parts = copy_for_each(shard, axis)
    return joined_along(parts, dim)


def sent_together(arrays, axis, dim, along):
    ends, at = ([], 0)
    for a in arrays[:-1]:
        at += a.shape[along]
        ends.append(at)
    both = jnp.concatenate(arrays, axis=along)
    return tuple(jnp.split(lax.all_gather(both, axis, axis=dim, tiled=True), ends, axis=along))


def split_up(shard, dim, count):
    before, after = (shard.shape[:dim], shard.shape[dim + 1 :])
    return jnp.moveaxis(shard.reshape(*before, count, -1, *after), dim, 0)


def sent_and_summed(shard, axis, dim):
    parts = split_up(shard, dim, lax.axis_size(axis))
    arrived = lax.all_to_all(parts, axis, split_axis=0, concat_axis=0, tiled=True)
    return arrived.sum(axis=0)


def side_by_side(arrays, axis, dim, along):
    columns = [a.reshape(*a.shape[:along], -1) for a in arrays]
    both = jnp.concatenate(columns, axis=along)
    out, at, done = (sent_and_summed(both, axis, dim), 0, [])
    for a, column in zip(arrays, columns):
        piece = out[..., at : at + column.shape[along]]
        done.append(piece.reshape(*piece.shape[:along], *a.shape[along:]))
        at += column.shape[along]
    return tuple(done)


def reduced_to_own(parts, axes, order):
    inside = parts.shape[1:]
    parts = parts.reshape(*(lax.axis_size(a) for a in axes), *inside)
    parts = jnp.moveaxis(parts, order, range(len(axes))).reshape(-1, *inside)
    for k in order:
        parts = lax.psum_scatter(parts, axes[k], scatter_dimension=0, tiled=True)
    return parts[0]


def sum_by_axis(shard, axes, order, dim):
    count = lax.axis_size(axes)
    return reduced_to_own(split_up(shard, dim, count), axes, order)


def one_axis_at_a_time(shard, axes):
    for axis in axes:
        shard = lax.psum(shard, axis)
    return shard


def per_device(
    lanczos_now,
    lanczos_prev,
    beta_prev,
    valence_energy,
    conduction_energy,
    valence_panel,
    conduction_panel,
    screened_coulomb,
    bare_coulomb,
):
    column_points = screened_coulomb.shape[1]
    wider = gather_directly(lanczos_now, COL, 2)
    vectors = lax.all_gather(wider, ROW, axis=1, tiled=True)
    products = jnp.einsum("pv,kvc->pkc", valence_panel, vectors, precision=precise)
    density = jnp.sum(products * conduction_panel[:, None, :], axis=2)
    pair_local = jnp.einsum("pc,kvc->pkv", conduction_panel, vectors, precision=precise)
    every_panel, every_density = sent_together((valence_panel, density), ROW_COL, 0, 1)
    first_point = lax.axis_index(COL) * column_points
    panel = lax.dynamic_slice_in_dim(every_panel, first_point, column_points, 0)
    far_density = lax.dynamic_slice_in_dim(every_density, first_point, column_points, 0)
    pair_terms = (
        jnp.einsum("mkv,nv->mkn", gather_directly(pair_local, COL, 0), panel, precision=precise)
        * screened_coulomb[:, None, :]
    )
    screened = jnp.einsum("mkn,nv->mkv", pair_terms, panel, precision=precise)
    potential = jnp.dot(bare_coulomb, far_density, precision=precise)
    direct_rows, local_potential = side_by_side((screened, potential), COL, 0, 2)
    weighted = local_potential[:, :, None] * conduction_panel[:, None, :]
    bare_term = jnp.einsum("pv,pkc->vkc", valence_panel, weighted, precision=precise)
    screened_term = jnp.einsum("mkv,mc->vkc", direct_rows, conduction_panel, precision=precise)
    band_rows = sum_by_axis(2.0 * bare_term - screened_term, ROW, (0, 2, 1), 0)
    kernel_part = sent_and_summed(band_rows, COL, 2)
    kernel_part = jnp.transpose(kernel_part, (1, 0, 2))
    gaps = conduction_energy[None, None, :] - valence_energy[None, :, None]
    image = gaps * lanczos_now + kernel_part
    inverse_size = 1.0 / (V * C)
    sum_qu, sum_qq, sum_uu, sum_up, sum_pp, sum_qp = (
        one_axis_at_a_time(jnp.sum(lanczos_now * image, axis=(1, 2)), ROW_COL),
        one_axis_at_a_time(jnp.sum(lanczos_now * lanczos_now, axis=(1, 2)), ROW_COL),
        one_axis_at_a_time(jnp.sum(image * image, axis=(1, 2)), ROW_COL),
        one_axis_at_a_time(jnp.sum(image * lanczos_prev, axis=(1, 2)), ROW_COL),
        one_axis_at_a_time(jnp.sum(lanczos_prev * lanczos_prev, axis=(1, 2)), ROW_COL),
        one_axis_at_a_time(jnp.sum(lanczos_now * lanczos_prev, axis=(1, 2)), ROW_COL),
    )
    coef_alpha = sum_qu * inverse_size / (sum_qq * inverse_size + epsilon)
    mean_ww = (
        sum_uu
        - 2.0 * coef_alpha * sum_qu
        - 2.0 * beta_prev * sum_up
        + coef_alpha * coef_alpha * sum_qq
        + beta_prev * beta_prev * sum_pp
        + 2.0 * coef_alpha * beta_prev * sum_qp
    ) * inverse_size
    resid = (
        image - coef_alpha[:, None, None] * lanczos_now - beta_prev[:, None, None] * lanczos_prev
    )
    beta_next = jnp.sqrt(mean_ww + epsilon)
    return (resid / beta_next[:, None, None], jnp.stack([coef_alpha, beta_next], axis=1))


def solution(mesh):
    torus = Mesh(mesh.devices.reshape(4, 2, 4, 4, 2), ("row_0", "row_1", "row_2", "col_0", "col_1"))
    return jax.shard_map(
        per_device,
        mesh=torus,
        in_specs=(
            P(None, ROW, COL),
            P(None, ROW, COL),
            P(),
            P(ROW),
            P(COL),
            P(ROW_COL, None),
            P(ROW_COL, None),
            P(ROW, COL),
            P(ROW, COL),
        ),
        out_specs=(P(None, ROW, COL), P()),
        check_vma=False,
    )
```

profile of v0, /device:TPU:1, one launch (start us, length us, event | category | flops | bytes accessed | tf_op | source)
XLA Modules:
  0.0 726.4 jit_solution(2510422371659446498)
XLA Ops:
  7.2 0.0 all-gather.3.cloned.1.call-start
  7.2 0.7 broadcast_in_dim.4
  7.9 12.2 %all_to_all.20 = f32[8,1,8,128]{3,2,1,0:T(8,128)} all-to-all(f32[8,1,8,128]{3,2,1,0:T(8,128)S(1)} %broadcast_in_dim.4), channel_id=1, replica_groups=mesh['row_0'=4,'row_1'=2,'row_2'=4,'col_0'=4,'col_1'=2] {'col_0','col_1'}, dimensions={0} | all-to-all | bytes 65536 | tf_op jit(solution)/shard_map/all_to_all | solution.py:18
  20.2 0.0 all-gather.3.cloned.1.call-update
  20.2 0.0 all-gather.5.cloned.1.call-start
  20.2 80.5 %all-gather.3.cloned.1.call-done = f32[1,256,1024]{2,1,0:T(8,128)} async-done(((f32[1,8,1024]{2,1,0:T(8,128)}), f32[1,256,1024]{2,1,0:T(8,128)}) %all-gather.3.cloned.1.call-update) | async-done | bytes 1048592 | tf_op jit(solution)/shard_map/all_gather | solution.py:96
  100.7 2.1 fusion.7
  102.9 0.1 copy.21
  103.0 1.5 pad_maximum_fusion.1
  104.5 0.0 all-gather.5.cloned.1.call-update
  104.5 2.4 fusion.9
  106.9 1.1 broadcast_in_dim.5
  108.0 5.7 all-to-all-start.1
  113.7 17.8 %all-to-all-done.1 = f32[8,64,1,256]{3,2,1,0:T(1,128)S(1)} async-done(((f32[8,64,1,256]{3,2,1,0:T(1,128)}), f32[8,64,1,256]{3,2,1,0:T(1,128)S(1)}, u32[]{:S(2)}, u32[]{:S(2)}) %all-to-all-start.1) | async-done | bytes 524320 | tf_op jit(solution)/shard_map/all_to_all | solution.py:18
  131.5 406.5 %all-gather.5.cloned.1.call-done = f32[16384,257]{1,0:T(8,128)} async-done(((f32[64,257]{1,0:T(8,128)}), f32[16384,257]{1,0:T(8,128)}) %all-gather.5.cloned.1.call-update) | async-done | bytes 16842768 | tf_op jit(solution)/shard_map/all_gather | solution.py:38
  538.1 3.4 slice-done
  541.4 0.3 dynamic-slice_reduce_fusion
  541.8 0.9 copy-done.1
  542.6 3.4 convolution_bitcast_fusion.1
  546.0 6.5 split.8
  552.5 0.0 copy-start.2
  552.5 3.6 fusion.3
  556.1 0.0 copy-start.3
  556.1 3.5 fusion
  559.6 0.1 pad_maximum_fusion
  559.7 27.3 %all_to_all.21 = f32[8,64,1,257]{3,1,2,0:T(8,128)S(1)} all-to-all(f32[8,64,1,257]{3,1,2,0:T(8,128)S(1)} %pad_maximum_fusion), channel_id=1, replica_groups=mesh['row_0'=4,'row_1'=2,'row_2'=4,'col_0'=4,'col_1'=2] {'col_0','col_1'}, dimensions={0} | all-to-all | bytes 1052672 | tf_op jit(solution)/shard_map/all_to_all | solution.py:48
  587.0 0.1 slice_reduce_fusion
  587.2 1.1 fusion.5
  588.2 1.1 fusion.6
  589.3 1.1 copy.25
  590.4 0.0 reduce-scatter.4.cloned.1.call-update
  590.4 0.0 reduce-scatter.6.cloned.1.call-start
  590.5 19.3 %reduce-scatter.4.cloned.1.call-done = f32[8,8,1,1024]{3,1,0,2:T(8,128)} async-done(((f32[32,8,1,1024]{3,1,0,2:T(8,128)}), f32[8,8,1,1024]{3,1,0,2:T(8,128)}) %reduce-scatter.4.cloned.1.call-update) | async-done | bytes 262160 | tf_op jit(solution)/shard_map/reduce_scatter | solution.py:68
  609.8 0.0 reduce-scatter.6.cloned.1.call-update
  609.8 0.0 reduce-scatter.8.cloned.1.call-start
  609.8 24.6 %reduce-scatter.6.cloned.1.call-done = f32[2,8,1,1024]{3,1,0,2:T(8,128)} async-done(((f32[8,8,1,1024]{3,1,0,2:T(8,128)}), f32[2,8,1,1024]{3,1,0,2:T(8,128)}) %reduce-scatter.6.cloned.1.call-update) | async-done | bytes 65552 | tf_op jit(solution)/shard_map/reduce_scatter | solution.py:68
  634.4 0.0 reduce-scatter.8.cloned.1.call-update
  634.5 24.0 %reduce-scatter.8.cloned.1.call-done = f32[1,8,1,1024]{3,1,0,2:T(8,128)} async-done(((f32[2,8,1,1024]{3,1,0,2:T(8,128)}), f32[1,8,1,1024]{3,1,0,2:T(8,128)}) %reduce-scatter.8.cloned.1.call-update) | async-done | bytes 32784 | tf_op jit(solution)/shard_map/reduce_scatter | solution.py:68
  658.4 3.7 all-to-all-start.3
  662.8 4.3 all-to-all-done.3
  667.2 0.8 multiply_reduce_fusion.2
  668.0 9.6 %all-reduce.2 = (f32[1]{0:T(128)}, f32[1]{0:T(128)}, f32[1]{0:T(128)}, f32[1]{0:T(128)}, f32[1]{0:T(128)}, /*index=5*/f32[1]{0:T(128)}) all-reduce(f32[1]{0:T(128)} %bitcast.30, f32[1]{0:T(128)} %bitcast.26, f32[1]{0:T(128)} %bitcast.27, f32[1]{0:T(128)} %bitcast.31, ...), channel_id=1, replica_groups=mesh['row_0'=4,'row_1'=2,'row_2'=4,'col_0'=4,'col_1'=2] {'row_0'}, use_global_device_ids=true, to_apply=%region_19.0 | all-reduce | flops 6 | bytes 48 | tf_op jit(solution)/shard_map/psum | solution.py:79
  677.5 8.4 %all-reduce.4 = (f32[1]{0:T(128)}, f32[1]{0:T(128)}, f32[1]{0:T(128)}, f32[1]{0:T(128)}, f32[1]{0:T(128)}, /*index=5*/f32[1]{0:T(128)}) all-reduce(f32[1]{0:T(128)} %get-tuple-element.20, f32[1]{0:T(128)} %get-tuple-element.21, f32[1]{0:T(128)} %get-tuple-element.22, ...), channel_id=1, replica_groups=mesh['row_0'=4,'row_1'=2,'row_2'=4,'col_0'=4,'col_1'=2] {'row_1'}, use_global_device_ids=true, to_apply=%region_20.0 | all-reduce | flops 6 | bytes 48 | tf_op jit(solution)/shard_map/psum | solution.py:79
  685.9 9.1 %all-reduce.1 = (f32[1]{0:T(128)}, f32[1]{0:T(128)}, f32[1]{0:T(128)}, f32[1]{0:T(128)}, f32[1]{0:T(128)}, /*index=5*/f32[1]{0:T(128)}) all-reduce(f32[1]{0:T(128)} %get-tuple-element.32, f32[1]{0:T(128)} %get-tuple-element.33, f32[1]{0:T(128)} %get-tuple-element.34, ...), channel_id=1, replica_groups=mesh['row_0'=4,'row_1'=2,'row_2'=4,'col_0'=4,'col_1'=2] {'row_2'}, use_global_device_ids=true, to_apply=%region_21.0 | all-reduce | flops 6 | bytes 48 | tf_op jit(solution)/shard_map/psum | solution.py:79
  695.1 7.8 %all-reduce = (f32[1]{0:T(128)}, f32[1]{0:T(128)}, f32[1]{0:T(128)}, f32[1]{0:T(128)}, f32[1]{0:T(128)}, /*index=5*/f32[1]{0:T(128)}) all-reduce(f32[1]{0:T(128)} %get-tuple-element.14, f32[1]{0:T(128)} %get-tuple-element.15, f32[1]{0:T(128)} %get-tuple-element.16, ...), channel_id=1, replica_groups=mesh['row_0'=4,'row_1'=2,'row_2'=4,'col_0'=4,'col_1'=2] {'col_0'}, use_global_device_ids=true, to_apply=%region_22.0 | all-reduce | flops 6 | bytes 48 | tf_op jit(solution)/shard_map/psum | solution.py:79
  702.9 10.7 %all-reduce.3 = (f32[1]{0:T(128)}, f32[1]{0:T(128)}, f32[1]{0:T(128)}, f32[1]{0:T(128)}, f32[1]{0:T(128)}, /*index=5*/f32[1]{0:T(128)}) all-reduce(f32[1]{0:T(128)} %get-tuple-element.8, f32[1]{0:T(128)} %get-tuple-element.9, f32[1]{0:T(128)} %get-tuple-element.10, ...), channel_id=1, replica_groups=mesh['row_0'=4,'row_1'=2,'row_2'=4,'col_0'=4,'col_1'=2] {'col_1'}, use_global_device_ids=true, to_apply=%region_23.0 | all-reduce | flops 6 | bytes 48 | tf_op jit(solution)/shard_map/psum | solution.py:79
  718.6 0.6 pad_maximum_fusion.2
  719.2 0.7 subtract_divide_fusion
  (18 shorter events, 0.1 us)
Async XLA Ops:
  7.2 93.6 %all-gather.3.cloned.1.call-start = ((), (), s32[]{:S(2)}) async-start(), calls=%async_computation.7 | async-start | bytes 1081344 | tf_op jit(solution)/shard_map/all_gather | solution.py:96
  20.2 517.9 %all-gather.5.cloned.1.call-start = ((), (), s32[]{:S(2)}) async-start(), calls=%async_computation.8 | async-start | bytes 25264128 | tf_op jit(solution)/shard_map/all_gather | solution.py:38
  108.0 23.5 %all-to-all-start.1 = ((f32[8,64,1,256]{3,2,1,0:T(1,128)}), f32[8,64,1,256]{3,2,1,0:T(1,128)S(1)}, u32[]{:S(2)}, u32[]{:S(2)}) async-start(f32[8,64,1,256]{3,2,1,0:T(1,128)} %broadcast_in_dim.5), calls=%async_computation.1 | async-start | bytes 1048576 | tf_op jit(solution)/shard_map/all_to_all | solution.py:18
  113.7 496.0 %reduce-scatter.4.cloned.1.call-start = ((), (), s32[]{:S(2)}) async-start(), calls=%async_computation.9 | async-start | bytes 1310720 | tf_op jit(solution)/shard_map/reduce_scatter | solution.py:68
  538.0 3.4 slice-start
  538.0 4.6 copy-start.1
  552.5 3.6 copy-start.2
  556.1 31.0 %copy-start.3 = (f32[64,256]{1,0:T(8,128)S(1)}, f32[64,256]{1,0:T(8,128)}, u32[]{:S(2)}) copy-start(f32[64,256]{1,0:T(8,128)} %param.14) | copy-start | bytes 196612
  559.6 27.6 %copy-start = (f32[64,1024]{1,0:T(8,128)S(1)}, f32[64,1024]{1,0:T(8,128)}, u32[]{:S(2)}) copy-start(f32[64,1024]{1,0:T(8,128)} %param.15) | copy-start | bytes 786436
  587.0 80.2 %copy-start.4 = (f32[1,8,128]{2,1,0:T(8,128)S(1)}, f32[1,8,128]{2,1,0:T(8,128)}, u32[]{:S(2)}) copy-start(f32[1,8,128]{2,1,0:T(8,128)} %param.9) | copy-start | bytes 12292
  587.0 80.2 %copy-start.5 = (f32[1,8,128]{2,1,0:T(8,128)S(1)}, f32[1,8,128]{2,1,0:T(8,128)}, u32[]{:S(2)}) copy-start(f32[1,8,128]{2,1,0:T(8,128)} %param.10) | copy-start | bytes 12292
  587.0 80.2 %copy-start.6 = (f32[8]{0:T(128)S(1)}, f32[8]{0:T(128)}, u32[]{:S(2)}) copy-start(f32[8]{0:T(128)} %param.12) | copy-start | bytes 100
  587.0 80.2 %copy-start.7 = (f32[128]{0:T(128)S(1)}, f32[128]{0:T(128)}, u32[]{:S(2)}) copy-start(f32[128]{0:T(128)} %param.13) | copy-start | bytes 1540
  590.4 44.0 %reduce-scatter.6.cloned.1.call-start = ((), (), s32[]{:S(2)}) async-start(), calls=%async_computation.10 | async-start | bytes 327680 | tf_op jit(solution)/shard_map/reduce_scatter | solution.py:68
  609.8 48.6 %reduce-scatter.8.cloned.1.call-start = ((), (), s32[]{:S(2)}) async-start(), calls=%async_computation.11 | async-start | bytes 98304 | tf_op jit(solution)/shard_map/reduce_scatter | solution.py:68
  658.4 8.7 %all-to-all-start.3 = ((f32[8,8,1,128]{3,1,2,0:T(8,128)}), f32[8,8,1,128]{3,1,2,0:T(8,128)S(1)}, u32[]{:S(2)}, u32[]{:S(2)}) async-start(f32[8,8,1,128]{3,1,2,0:T(8,128)} %bitcast.88), calls=%async_computation.6 | async-start | bytes 65536 | tf_op jit(solution)/shard_map/all_to_all | solution.py:48
Sparse Core Ops, SparseCore 0:
  20.3 80.3 all-gather.2
  104.6 433.3 all-gather.4
  590.5 19.1 reduce-scatter.3
  612.1 22.2 reduce-scatter.5
  636.7 21.6 reduce-scatter.7
where the time goes:
time: 727 us; the launch traced here: 726 us
  waiting for transfers between devices  577 us (79%)
  blocking collectives  85.2 us (12%)
  between operations  19.6 us (3%)
  matrix products  17 us (2%)
  local copies, waits for them, and re-layouts  14.3 us (2%)
  starting transfers between devices  9.62 us (1%)
    all_gather x1, waiting for transfers between devices, sent_together(): lax.all_gather(both, axis, axis=dim, tiled=True)  407 us
    all_gather x1, waiting for transfers between devices, per_device(): vectors = lax.all_gather(wider, ROW, axis=1, tiled=True)  80.5 us
    reduce_scatter x3, waiting for transfers between devices, reduced_to_own(): parts = lax.psum_scatter(parts, axes[k], scatter_dimension=0, tiled=True)  67.8 us
    psum x5, blocking collectives, one_axis_at_a_time(): shard = lax.psum(shard, axis)  45.6 us
    all_to_all x1, blocking collectives, sent_and_summed(): lax.all_to_all(parts, axis, split_axis=0, concat_axis=0, tiled=True)  27.3 us
    all_to_all x1, waiting for transfers between devices, copy_for_each(): return lax.all_to_all(copies, axis, split_axis=0, concat_axis=0, tiled=True)  17.8 us
  transfers between devices with their start and end apart: 7, of which 7 were waited for; matrix products, arithmetic and copies ran while one was open for 0% of the time, Pallas kernels for 0%

commit v1 on v0

--- a/solution.py
+++ b/solution.py
@@ -76,7 +76,7 @@
 
 def one_axis_at_a_time(shard, axes):
     for axis in axes:
-        shard = lax.psum(shard, axis)
+        shard = jnp.sum(lax.all_gather(shard, axis), axis=0)
     return shard
 
 

time: 727 us -> 785 us (1.080)
  local copies, waits for them, and re-layouts: 14.3 us -> 58.3 us
  other arithmetic: 3.62 us -> 21.6 us
    psum x5 -> x0, blocking collectives: 45.6 us -> none  [one_axis_at_a_time(): shard = lax.psum(shard, axis)]
    unnamed x17 -> x92, local copies, waits for them, and re-layouts: 0.93 us -> 44.9 us
    unnamed x0 -> x5, blocking collectives: none -> 42.1 us
    reduce_sum x0 -> x30, other arithmetic: none -> 18 us  [one_axis_at_a_time(): shard = jnp.sum(lax.all_gather(shard, axis), axis=0)]
  transfers between devices with their start and end apart: 7 -> 7, of which waited for: 7 -> 7; matrix products, arithmetic and copies ran while one was open for 0% -> 1% of each run, Pallas kernels for 0% -> 0%
where the time goes in v1:
time: 785 us; the launch traced here: 784 us
  waiting for transfers between devices  576 us (73%)
  blocking collectives  81.6 us (10%)
  local copies, waits for them, and re-layouts  58.3 us (7%)
  other arithmetic  21.6 us (3%)
  between operations  20 us (3%)
  matrix products  17 us (2%)
  starting transfers between devices  9.62 us (1%)
    all_gather x1, waiting for transfers between devices, sent_together(): lax.all_gather(both, axis, axis=dim, tiled=True)  407 us
    all_gather x1, waiting for transfers between devices, per_device(): vectors = lax.all_gather(wider, ROW, axis=1, tiled=True)  80.5 us
    reduce_scatter x3, waiting for transfers between devices, reduced_to_own(): parts = lax.psum_scatter(parts, axes[k], scatter_dimension=0, tiled=True)  67.9 us
    unnamed x92, local copies, waits for them, and re-layouts  44.9 us
    unnamed x5, blocking collectives  42.1 us
    all_to_all x1, blocking collectives, sent_and_summed(): lax.all_to_all(parts, axis, split_axis=0, concat_axis=0, tiled=True)  27.3 us
    reduce_sum x30, other arithmetic, one_axis_at_a_time(): shard = jnp.sum(lax.all_gather(shard, axis), axis=0)  18 us
    all_to_all x1, waiting for transfers between devices, copy_for_each(): return lax.all_to_all(copies, axis, split_axis=0, concat_axis=0, tiled=True)  17.8 us
  transfers between devices with their start and end apart: 7, of which 7 were waited for; matrix products, arithmetic and copies ran while one was open for 1% of the time, Pallas kernels for 0%

profile of v1, /device:TPU:1, one launch (start us, length us, event | category | flops | bytes accessed | tf_op | source)
XLA Modules:
  0.0 784.0 jit_solution(13575576369869841500)
XLA Ops:
  7.9 12.2 %all_to_all.20 = f32[8,1,8,128]{3,2,1,0:T(8,128)} all-to-all(f32[8,1,8,128]{3,2,1,0:T(8,128)S(1)} %broadcast_in_dim.4), channel_id=1, replica_groups=mesh['row_0'=4,'row_1'=2,'row_2'=4,'col_0'=4,'col_1'=2] {'col_0','col_1'}, dimensions={0} | all-to-all | bytes 65536 | tf_op jit(solution)/shard_map/all_to_all | solution.py:18
  20.2 80.5 %all-gather.3.cloned.1.call-done = f32[1,256,1024]{2,1,0:T(8,128)} async-done(((f32[1,8,1024]{2,1,0:T(8,128)}), f32[1,256,1024]{2,1,0:T(8,128)}) %all-gather.3.cloned.1.call-update) | async-done | bytes 1048592 | tf_op jit(solution)/shard_map/all_gather | solution.py:96
  100.7 2.1 fusion.7
  103.0 1.5 pad_maximum_fusion.1
  104.5 2.4 fusion.9
  108.0 5.7 all-to-all-start.1
  113.7 17.8 %all-to-all-done.1 = f32[8,64,1,256]{3,2,1,0:T(1,128)S(1)} async-done(((f32[8,64,1,256]{3,2,1,0:T(1,128)}), f32[8,64,1,256]{3,2,1,0:T(1,128)S(1)}, u32[]{:S(2)}, u32[]{:S(2)}) %all-to-all-start.1) | async-done | bytes 524320 | tf_op jit(solution)/shard_map/all_to_all | solution.py:18
  131.5 406.5 %all-gather.5.cloned.1.call-done = f32[16384,257]{1,0:T(8,128)} async-done(((f32[64,257]{1,0:T(8,128)}), f32[16384,257]{1,0:T(8,128)}) %all-gather.5.cloned.1.call-update) | async-done | bytes 16842768 | tf_op jit(solution)/shard_map/all_gather | solution.py:38
  538.1 3.4 slice-done
  542.6 3.4 convolution_bitcast_fusion.1
  546.0 6.5 split.8
  552.5 3.6 fusion.3
  556.1 3.5 fusion
  559.7 27.3 %all_to_all.21 = f32[8,64,1,257]{3,1,2,0:T(8,128)S(1)} all-to-all(f32[8,64,1,257]{3,1,2,0:T(8,128)S(1)} %pad_maximum_fusion), channel_id=1, replica_groups=mesh['row_0'=4,'row_1'=2,'row_2'=4,'col_0'=4,'col_1'=2] {'col_0','col_1'}, dimensions={0} | all-to-all | bytes 1052672 | tf_op jit(solution)/shard_map/all_to_all | solution.py:48
  590.5 19.3 %reduce-scatter.4.cloned.1.call-done = f32[8,8,1,1024]{3,1,0,2:T(8,128)} async-done(((f32[32,8,1,1024]{3,1,0,2:T(8,128)}), f32[8,8,1,1024]{3,1,0,2:T(8,128)}) %reduce-scatter.4.cloned.1.call-update) | async-done | bytes 262160 | tf_op jit(solution)/shard_map/reduce_scatter | solution.py:68
  609.9 24.6 %reduce-scatter.6.cloned.1.call-done = f32[2,8,1,1024]{3,1,0,2:T(8,128)} async-done(((f32[8,8,1,1024]{3,1,0,2:T(8,128)}), f32[2,8,1,1024]{3,1,0,2:T(8,128)}) %reduce-scatter.6.cloned.1.call-update) | async-done | bytes 65552 | tf_op jit(solution)/shard_map/reduce_scatter | solution.py:68
  634.5 24.0 %reduce-scatter.8.cloned.1.call-done = f32[1,8,1,1024]{3,1,0,2:T(8,128)} async-done(((f32[2,8,1,1024]{3,1,0,2:T(8,128)}), f32[1,8,1,1024]{3,1,0,2:T(8,128)}) %reduce-scatter.8.cloned.1.call-update) | async-done | bytes 32784 | tf_op jit(solution)/shard_map/reduce_scatter | solution.py:68
  658.5 3.7 all-to-all-start.3
  664.1 3.1 all-to-all-done.3
  668.0 1.4 dynamic-update-slice.10
  669.4 1.3 dynamic-update-slice
  672.1 1.4 dynamic-update-slice.15
  673.5 1.4 dynamic-update-slice.20
  674.8 1.4 dynamic-update-slice.25
  676.8 8.9 %all-reduce.32 = (f32[4]{0:T(128)S(1)}, f32[4]{0:T(128)S(1)}, f32[4]{0:T(128)S(1)}, f32[4]{0:T(128)S(1)}, f32[4]{0:T(128)S(1)}, /*index=5*/f32[4]{0:T(128)S(1)}) all-reduce(f32[4]{0:T(128)S(1)} %dynamic-update-slice.10, f32[4]{0:T(128)S(1)} %dynamic-update-slice, ...), channel_id=1, replica_groups=mesh['row_0'=4,'row_1'=2,'row_2'=4,'col_0'=4,'col_1'=2] {'row_0'}, use_global_device_ids=true, to_apply=%add.10 | all-reduce | flops 24 | bytes 192
  686.9 1.3 dynamic-update-slice.11
  688.2 1.3 dynamic-update-slice.1
  690.1 1.3 dynamic-update-slice.6
  692.0 1.3 dynamic-update-slice.16
  693.9 1.3 dynamic-update-slice.21
  697.8 7.7 all-reduce.34
  706.6 1.4 dynamic-update-slice.12
  708.1 1.4 dynamic-update-slice.2
  710.1 1.4 dynamic-update-slice.7
  712.2 1.4 dynamic-update-slice.17
  714.2 1.4 dynamic-update-slice.22
  716.3 1.4 dynamic-update-slice.27
  718.3 8.5 %all-reduce.31 = (f32[4]{0:T(128)S(1)}, f32[4]{0:T(128)S(1)}, f32[4]{0:T(128)S(1)}, f32[4]{0:T(128)S(1)}, f32[4]{0:T(128)S(1)}, /*index=5*/f32[4]{0:T(128)S(1)}) all-reduce(f32[4]{0:T(128)S(1)} %dynamic-update-slice.12, f32[4]{0:T(128)S(1)} %dynamic-update-slice.2, ...), channel_id=1, replica_groups=mesh['row_0'=4,'row_1'=2,'row_2'=4,'col_0'=4,'col_1'=2] {'row_2'}, use_global_device_ids=true, to_apply=%add.12 | all-reduce | flops 24 | bytes 192
  728.0 1.4 dynamic-update-slice.13
  729.4 1.4 dynamic-update-slice.3
  731.4 1.4 dynamic-update-slice.8
  733.4 1.4 dynamic-update-slice.18
  735.4 1.4 dynamic-update-slice.23
  737.4 1.4 dynamic-update-slice.28
  738.8 7.1 all-reduce.30
  748.4 1.3 dynamic-update-slice.4
  754.1 1.3 dynamic-update-slice.24
  757.4 9.9 %all-reduce.33 = (f32[2]{0:T(128)S(1)}, f32[2]{0:T(128)S(1)}, f32[2]{0:T(128)S(1)}, f32[2]{0:T(128)S(1)}, f32[2]{0:T(128)S(1)}, /*index=5*/f32[2]{0:T(128)S(1)}) all-reduce(f32[2]{0:T(128)S(1)} %dynamic-update-slice.14, f32[2]{0:T(128)S(1)} %dynamic-update-slice.4, ...), channel_id=1, replica_groups=mesh['row_0'=4,'row_1'=2,'row_2'=4,'col_0'=4,'col_1'=2] {'col_1'}, use_global_device_ids=true, to_apply=%add.14 | all-reduce | flops 12 | bytes 96
  (123 shorter events, 37.8 us)
Async XLA Ops:
  7.2 93.6 %all-gather.3.cloned.1.call-start = ((), (), s32[]{:S(2)}) async-start(), calls=%async_computation.7 | async-start | bytes 1081344 | tf_op jit(solution)/shard_map/all_gather | solution.py:96
  20.2 517.9 %all-gather.5.cloned.1.call-start = ((), (), s32[]{:S(2)}) async-start(), calls=%async_computation.8 | async-start | bytes 25264128 | tf_op jit(solution)/shard_map/all_gather | solution.py:38
  108.0 23.5 %all-to-all-start.1 = ((f32[8,64,1,256]{3,2,1,0:T(1,128)}), f32[8,64,1,256]{3,2,1,0:T(1,128)S(1)}, u32[]{:S(2)}, u32[]{:S(2)}) async-start(f32[8,64,1,256]{3,2,1,0:T(1,128)} %broadcast_in_dim.5), calls=%async_computation.1 | async-start | bytes 1048576 | tf_op jit(solution)/shard_map/all_to_all | solution.py:18
  113.7 496.1 %reduce-scatter.4.cloned.1.call-start = ((), (), s32[]{:S(2)}) async-start(), calls=%async_computation.9 | async-start | bytes 1310720 | tf_op jit(solution)/shard_map/reduce_scatter | solution.py:68
  538.0 3.4 slice-start
  538.0 4.6 copy-start.1
  552.5 3.6 copy-start.2
  556.1 31.1 %copy-start.3 = (f32[64,256]{1,0:T(8,128)S(1)}, f32[64,256]{1,0:T(8,128)}, u32[]{:S(2)}) copy-start(f32[64,256]{1,0:T(8,128)} %param.14) | copy-start | bytes 196612
  559.6 27.6 %copy-start = (f32[64,1024]{1,0:T(8,128)S(1)}, f32[64,1024]{1,0:T(8,128)}, u32[]{:S(2)}) copy-start(f32[64,1024]{1,0:T(8,128)} %param.15) | copy-start | bytes 786436
  587.0 75.3 %copy-start.12 = (u32[256]{0:T(256)S(1)}, u32[256]{0:T(256)}, u32[]{:S(2)}) copy-start(u32[256]{0:T(256)} %constant.33) | copy-start | bytes 3076
  587.0 75.9 %copy-start.11 = (u32[256]{0:T(256)S(1)}, u32[256]{0:T(256)}, u32[]{:S(2)}) copy-start(u32[256]{0:T(256)} %constant.38) | copy-start | bytes 3076
  587.0 76.4 %copy-start.10 = (u32[256]{0:T(256)S(1)}, u32[256]{0:T(256)}, u32[]{:S(2)}) copy-start(u32[256]{0:T(256)} %constant.43) | copy-start | bytes 3076
  587.0 80.3 %copy-start.4 = (f32[1,8,128]{2,1,0:T(8,128)S(1)}, f32[1,8,128]{2,1,0:T(8,128)}, u32[]{:S(2)}) copy-start(f32[1,8,128]{2,1,0:T(8,128)} %param.9) | copy-start | bytes 12292
  587.0 80.3 %copy-start.5 = (f32[1,8,128]{2,1,0:T(8,128)S(1)}, f32[1,8,128]{2,1,0:T(8,128)}, u32[]{:S(2)}) copy-start(f32[1,8,128]{2,1,0:T(8,128)} %param.10) | copy-start | bytes 12292
  587.0 80.3 %copy-start.6 = (f32[8]{0:T(128)S(1)}, f32[8]{0:T(128)}, u32[]{:S(2)}) copy-start(f32[8]{0:T(128)} %param.12) | copy-start | bytes 100
  587.0 80.3 %copy-start.7 = (f32[128]{0:T(128)S(1)}, f32[128]{0:T(128)}, u32[]{:S(2)}) copy-start(f32[128]{0:T(128)} %param.13) | copy-start | bytes 1540
  587.0 89.2 %copy-start.9 = (u32[256]{0:T(256)S(1)}, u32[256]{0:T(256)}, u32[]{:S(2)}) copy-start(u32[256]{0:T(256)} %constant.48) | copy-start | bytes 3076
  587.0 110.1 %copy-start.8 = (u32[256]{0:T(256)S(1)}, u32[256]{0:T(256)}, u32[]{:S(2)}) copy-start(u32[256]{0:T(256)} %constant.53) | copy-start | bytes 3076
  590.5 44.0 %reduce-scatter.6.cloned.1.call-start = ((), (), s32[]{:S(2)}) async-start(), calls=%async_computation.10 | async-start | bytes 327680 | tf_op jit(solution)/shard_map/reduce_scatter | solution.py:68
  609.8 48.7 %reduce-scatter.8.cloned.1.call-start = ((), (), s32[]{:S(2)}) async-start(), calls=%async_computation.11 | async-start | bytes 98304 | tf_op jit(solution)/shard_map/reduce_scatter | solution.py:68
  658.5 8.7 %all-to-all-start.3 = ((f32[8,8,1,128]{3,1,2,0:T(8,128)}), f32[8,8,1,128]{3,1,2,0:T(8,128)S(1)}, u32[]{:S(2)}, u32[]{:S(2)}) async-start(f32[8,8,1,128]{3,1,2,0:T(8,128)} %bitcast.123), calls=%async_computation.6 | async-start | bytes 65536 | tf_op jit(solution)/shard_map/all_to_all | solution.py:48
Sparse Core Ops, SparseCore 0:
  20.3 80.3 all-gather.2
  104.6 433.3 all-gather.4
  590.6 19.1 reduce-scatter.3
  612.2 22.2 reduce-scatter.5
  636.8 21.6 reduce-scatter.7
